TPU v7x, 512 devices: a whole 4x4x16 slice. The times are simulated.
512 devices in a mesh: contract: 32 (over z, y_lo), out: 16 (over y_hi, x, core).
Axes of the slice: x: 4, y: 4 (y_hi: 2, y_lo: 2; y = y_hi * 2 + y_lo), z: 16, core: 2. Of those that a mesh axis runs over, the one named last changes fastest.
Arguments:
- chol: bfloat16 [128, 1024, 640], P('out', 'contract'), may hold values from -1.1953125 to 1.1953125
- amplitudes: bfloat16 [128, 32768], P('out', 'contract'), may hold values from -0.0625 to 0.0625
- tile_pairs: int32 [64, 2], replicated, may hold values from 0 to 7, as said below
- partner: int32 [64], replicated, may hold values from 0 to 63, as said below
- pair_swap: int32 [128], replicated, may hold values from 0 to 127, as said below
Outputs:
- residual: float32 [64, 128, 256], P('out', 'contract')
Inputs may be any that keep to these rules, and one draw needn't show every extreme that they name: `tile_pairs`: each ordered pair of tiles of 0 to 7 stands at exactly one slot. partner[s] is the slot holding the pair of slot s reversed; a diagonal pair is its own partner. `pair_swap`: an involution without fixed points that maps each aligned block of 4 pairs into itself.
All inputs are finite; a program needn't handle non-finite values.
Results may differ from a plain program's by a relative error of at most 0.0029.
Values may be sent and summed in bfloat16 or wider, within the bound.
No kernel may reach another device: no remote copies, remote signals or barrier semaphores. Data moves between devices by JAX's collectives and lax.ppermute only.
A program may use at most 128 MiB of HBM per device.

v0:
```python
import jax
import jax.numpy as jnp
from jax import lax
from jax.sharding import Mesh
from jax.sharding import PartitionSpec as P

TS = 16
CONTRACT = ("contract_0", "contract_1")


def broadcast_by_axis(array, axes, root):
    array = jnp.where(lax.axis_index(axes) == root, array, jnp.zeros_like(array))
    for axis in axes:
        array = lax.psum(array, axis)
    return array


def cut_along(array, dim, count):
    before, after = (array.shape[:dim], array.shape[dim + 1 :])
    return jnp.moveaxis(array.reshape(*before, count, -1, *after), dim, 0)


def sum_at_owner(array, axis, dim):
    count = lax.axis_size(axis)
    parts = lax.all_to_all(cut_along(array, dim, count), axis, 0, 0, tiled=True)
    return jnp.sum(parts, axis=0)


def laid_out(parts, dim):
    lengths = list(parts.shape[1:])
    lengths[dim] *= parts.shape[0]
    return jnp.moveaxis(parts, 0, dim).reshape(lengths)


def sent_to_all(array, axis):
    count = lax.axis_size(axis)
    return lax.all_to_all(
        jnp.broadcast_to(array[None], (count, *array.shape)), axis, 0, 0, tiled=True
    )


def collect(array, axis, dim):
    return laid_out(sent_to_all(array, axis), dim)


def pick_tile(source, tile):
    return lax.dynamic_slice_in_dim(source, tile * TS, TS, 0)


def on_device(chol, amplitudes, tile_pairs, partner, pair_swap):
    out_count = lax.axis_size("out")
    con_count = lax.axis_size(CONTRACT)
    out_index = lax.axis_index("out")
    con_index = lax.axis_index(CONTRACT)
    local_window = broadcast_by_axis(chol, CONTRACT, 0)
    rows_all, window, amps_all = (
        lax.all_gather(chol, "out", axis=0, tiled=True),
        lax.all_gather(local_window, "out", axis=0, tiled=True),
        lax.all_gather(amplitudes, "out", axis=0, tiled=True),
    )
    slot_count = tile_pairs.shape[0] // out_count
    first = out_index * slot_count
    pairs = lax.dynamic_slice_in_dim(tile_pairs, first, slot_count, 0)
    left = jax.vmap(pick_tile, (None, 0))(rows_all, pairs[:, 0])
    right = jax.vmap(pick_tile, (None, 0))(window, pairs[:, 1])
    integral = jnp.einsum(
        "sacp,sbdp->sabcd", left, right, preferred_element_type=jnp.float32
    ).astype(jnp.bfloat16)
    flat = integral.reshape(slot_count * TS * TS, -1)
    occ_dev = amps_all.shape[0] // con_count
    ladder = sum_at_owner(
        lax.dot_general(
            amps_all, flat, (((1,), (1,)), ((), ())), preferred_element_type=jnp.float32
        ),
        CONTRACT,
        0,
    )
    ladder = jnp.transpose(ladder.reshape(occ_dev, slot_count, TS, TS), (1, 0, 2, 3))
    own_swap = (
        lax.dynamic_slice_in_dim(pair_swap, con_index * occ_dev, occ_dev, 0) - con_index * occ_dev
    )
    turned = jnp.transpose(jnp.take(ladder, own_swap, axis=1), (0, 1, 3, 2))
    turned = turned.reshape(slot_count, occ_dev, TS * TS)
    every = collect(turned, "out", 0)
    wanted = lax.dynamic_slice_in_dim(partner, first, slot_count, 0)
    mirror = jnp.take(every, wanted, axis=0)
    return ladder.reshape(slot_count, occ_dev, TS * TS) + mirror


def solution(mesh):
    torus = Mesh(
        mesh.devices.reshape(16, 2, mesh.shape["out"]), ("contract_0", "contract_1", "out")
    )
    in_specs = (P("out", CONTRACT, None), P("out", CONTRACT), P(), P(), P())
    out_specs = P("out", CONTRACT, None)
    return jax.shard_map(
        on_device, mesh=torus, in_specs=in_specs, out_specs=out_specs, check_vma=False
    )
```

profile of v0, /device:TPU:1, one launch (start us, length us, event | category | flops | bytes accessed | tf_op | source)
XLA Modules:
  0.0 417.8 jit_solution(8291045161352591324)
XLA Ops:
  7.4 0.0 copy-start
  7.4 0.0 all-reduce.5.cloned.1.call-start
  7.4 1.7 broadcast_select_fusion
  9.1 0.0 all-reduce.5.cloned.1.call-update
  9.1 0.0 all-reduce.7.cloned.1.call-start
  9.2 133.9 %all-reduce.5.cloned.1.call-done = bf16[8,32,640]{2,1,0:T(8,128)(2,1)} async-done(((bf16[8,32,640]{2,1,0:T(8,128)(2,1)}), bf16[8,32,640]{2,1,0:T(8,128)(2,1)}) %all-reduce.5.cloned.1.call-update) | async-done | bytes 327696 | tf_op jit(solution)/shard_map/psum | solution.py:14
  143.0 0.0 all-reduce.7.cloned.1.call-update
  143.1 0.0 all-gather.5.cloned.1.call-start
  143.1 0.5 all-gather.5.cloned.1.call-update
  143.6 0.0 all-gather.3.cloned.1.call-start
  143.7 55.1 %all-reduce.7.cloned.1.call-done = bf16[8,32,640]{2,1,0:T(8,128)(2,1)} async-done(((bf16[8,32,640]{2,1,0:T(8,128)(2,1)}), bf16[8,32,640]{2,1,0:T(8,128)(2,1)}) %all-reduce.7.cloned.1.call-update) | async-done | bytes 327696 | tf_op jit(solution)/shard_map/psum | solution.py:14
  198.8 0.0 all-gather.3.cloned.1.call-update
  198.8 0.0 copy-done
  198.8 0.1 constant_dynamic-slice_fusion
  198.9 25.7 %all_gather.11 = bf16[128,1024]{1,0:T(8,128)(2,1)S(1)} all-gather(bf16[8,1024]{1,0:T(8,128)(2,1)} %param.6), channel_id=1, replica_groups=mesh['contract_0'=16,'contract_1'=2,'out'=16] {'out'}, dimensions={0}, use_global_device_ids=true | all-gather | bytes 278528 | tf_op jit(solution)/shard_map/all_gather | solution.py:59
  224.6 4.9 %all-gather.5.cloned.1.call-done = bf16[128,32,640]{2,1,0:T(8,128)(2,1)} async-done(((bf16[8,32,640]{2,1,0:T(8,128)(2,1)}), bf16[128,32,640]{2,1,0:T(8,128)(2,1)}) %all-gather.5.cloned.1.call-update) | async-done | bytes 5242896 | tf_op jit(solution)/shard_map/all_gather | solution.py:57
  229.5 3.5 gather_fusion.1
  233.0 74.3 %all-gather.3.cloned.1.call-done = bf16[128,32,640]{2,1,0:T(8,128)(2,1)} async-done(((bf16[8,32,640]{2,1,0:T(8,128)(2,1)}), bf16[128,32,640]{2,1,0:T(8,128)(2,1)}) %all-gather.3.cloned.1.call-update) | async-done | bytes 5242896 | tf_op jit(solution)/shard_map/all_gather | solution.py:58
  307.3 4.9 %gather_fusion = bf16[4,16,32,640]{3,2,1,0:T(8,128)(2,1)} fusion(bf16[128,32,640]{2,1,0:T(8,128)(2,1)} %all-gather.3.cloned.1.call-done, s32[4]{0:T(128)S(1)} %get-tuple-element.9), kind=kCustom, calls=%fused_computation | custom fusion | bytes 5242928 | tf_op jit(solution)/shard_map/vmap()/gather | solution.py:47
  312.3 10.4 %convert_bitcast_fusion = bf16[4,16,16,32,32]{3,4,1,2,0:T(8,128)(2,1)} fusion(bf16[4,16,32,640]{3,2,1,0:T(8,128)(2,1)S(1)} %gather_fusion.1, bf16[4,16,32,640]{3,2,1,0:T(8,128)(2,1)} %gather_fusion), kind=kOutput, calls=%fused_computation.4 | convolution fusion | flops 1343225856 | bytes 7340032 | tf_op jit(solution)/shard_map/sacp,sbdp->sabcd/dot_general | solution.py:66
  322.6 11.5 %copy.9 = bf16[4,16,16,32,32]{4,3,2,1,0:T(8,128)(2,1)} copy(bf16[4,16,16,32,32]{3,4,1,2,0:T(8,128)(2,1)} %convert_bitcast_fusion) | data formatting | bytes 4194304 | tf_op jit(solution)/shard_map/convert_element_type | solution.py:68
  334.1 11.3 %reshape.26 = bf16[1024,1024]{1,0:T(8,128)(2,1)S(1)} reshape(bf16[4,16,16,32,32]{4,3,2,1,0:T(8,128)(2,1)} %copy.9) | data formatting | bytes 4194304 | tf_op jit(solution)/shard_map/reshape | solution.py:69
  345.4 0.0 copy-start.1
  345.4 0.8 convolution_bitcast_fusion
  346.3 0.0 copy-start.2
  346.3 0.9 reshape.27
  347.2 12.3 %all-to-all-start = ((f32[32,4,1024]{2,1,0:T(4,128)}), f32[32,4,1024]{2,1,0:T(4,128)S(1)}, u32[]{:S(2)}, u32[]{:S(2)}) async-start(f32[32,4,1024]{2,1,0:T(4,128)} %reshape.27), calls=%async_computation | async-start | bytes 1048576 | tf_op jit(solution)/shard_map/all_to_all | solution.py:25
  359.6 0.0 copy-done.1
  359.6 0.1 compare_and_fusion
  359.7 32.0 %all-to-all-done = f32[32,4,1024]{2,1,0:T(4,128)S(1)} async-done(((f32[32,4,1024]{2,1,0:T(4,128)}), f32[32,4,1024]{2,1,0:T(4,128)S(1)}, u32[]{:S(2)}, u32[]{:S(2)}) %all-to-all-start) | async-done | bytes 524320 | tf_op jit(solution)/shard_map/all_to_all | solution.py:25
  391.7 0.1 reduce_sum.9
  391.8 0.1 reshape.28
  391.9 0.6 gather_fusion.2
  392.5 0.1 select_bitcast_fusion
  392.6 0.1 copy.11
  392.7 0.1 broadcast_in_dim.41
  392.8 0.8 broadcast_in_dim.42
  393.5 6.8 %all-to-all-start.1 = ((f32[16,4,4,256]{3,2,1,0:T(4,128)}), f32[16,4,4,256]{3,2,1,0:T(4,128)S(1)}, u32[]{:S(2)}, u32[]{:S(2)}) async-start(f32[16,4,4,256]{3,2,1,0:T(4,128)} %broadcast_in_dim.42), calls=%async_computation.1 | async-start | bytes 524288 | tf_op jit(solution)/shard_map/all_to_all | solution.py:37
  400.4 0.0 copy-done.2
  400.4 0.1 compare_and_fusion.1
  400.5 0.1 reshape.63
  400.6 8.5 %all-to-all-done.1 = f32[16,4,4,256]{3,2,1,0:T(4,128)S(1)} async-done(((f32[16,4,4,256]{3,2,1,0:T(4,128)}), f32[16,4,4,256]{3,2,1,0:T(4,128)S(1)}, u32[]{:S(2)}, u32[]{:S(2)}) %all-to-all-start.1) | async-done | bytes 262176 | tf_op jit(solution)/shard_map/all_to_all | solution.py:37
  409.1 0.6 gather_fusion.3
  409.6 0.7 copy_add_fusion
  (3 shorter events, 0.0 us)
Async XLA Ops:
  7.4 191.4 %copy-start = (s32[64,2]{0,1:T(2,128)S(1)}, s32[64,2]{0,1:T(2,128)}, u32[]{:S(2)}) copy-start(s32[64,2]{0,1:T(2,128)} %param.7) | copy-start | bytes 1540
  7.4 135.7 %all-reduce.5.cloned.1.call-start = ((), (), s32[]{:S(2)}) async-start(), calls=%async_computation.2 | async-start | bytes 655360 | tf_op jit(solution)/shard_map/psum | solution.py:14
  9.1 189.6 %all-reduce.7.cloned.1.call-start = ((), (), s32[]{:S(2)}) async-start(), calls=%async_computation.3 | async-start | bytes 655360 | tf_op jit(solution)/shard_map/psum | solution.py:14
  143.1 86.4 %all-gather.5.cloned.1.call-start = ((), (), s32[]{:S(2)}) async-start(), calls=%async_computation.5 | async-start | bytes 5570560 | tf_op jit(solution)/shard_map/all_gather | solution.py:57
  143.6 163.7 %all-gather.3.cloned.1.call-start = ((), (), s32[]{:S(2)}) async-start(), calls=%async_computation.4 | async-start | bytes 5570560 | tf_op jit(solution)/shard_map/all_gather | solution.py:58
  345.4 14.1 %copy-start.1 = (s32[128]{0:T(128)S(1)}, s32[128]{0:T(128)}, u32[]{:S(2)}) copy-start(s32[128]{0:T(128)} %param.9) | copy-start | bytes 1540
  346.3 54.1 %copy-start.2 = (s32[64]{0:T(128)S(1)}, s32[64]{0:T(128)}, u32[]{:S(2)}) copy-start(s32[64]{0:T(128)} %param.8) | copy-start | bytes 772
  347.2 44.5 %all-to-all-start = ((f32[32,4,1024]{2,1,0:T(4,128)}), f32[32,4,1024]{2,1,0:T(4,128)S(1)}, u32[]{:S(2)}, u32[]{:S(2)}) async-start(f32[32,4,1024]{2,1,0:T(4,128)} %reshape.27), calls=%async_computation | async-start | bytes 1048576 | tf_op jit(solution)/shard_map/all_to_all | solution.py:25
  393.5 15.5 %all-to-all-start.1 = ((f32[16,4,4,256]{3,2,1,0:T(4,128)}), f32[16,4,4,256]{3,2,1,0:T(4,128)S(1)}, u32[]{:S(2)}, u32[]{:S(2)}) async-start(f32[16,4,4,256]{3,2,1,0:T(4,128)} %broadcast_in_dim.42), calls=%async_computation.1 | async-start | bytes 524288 | tf_op jit(solution)/shard_map/all_to_all | solution.py:37
Sparse Core Ops, SparseCore 0:
  10.5 132.4 all-reduce.4
  145.9 52.8 all-reduce.6
Sparse Core Ops, SparseCore 1:
  146.8 82.6 all-gather.4
  232.7 74.6 all-gather.2
where the time goes:
time: 419 us; the launch traced here: 418 us
  waiting for transfers between devices  309 us (74%)
  local copies, waits for them, and re-layouts  34.5 us (8%)
  blocking collectives  25.7 us (6%)
  starting transfers between devices  19.3 us (5%)
  between operations  15 us (4%)
  matrix products  11.2 us (3%)
    psum x2, waiting for transfers between devices, broadcast_by_axis(): array = lax.psum(array, axis)  189 us
    all_gather x1, waiting for transfers between devices, on_device(): lax.all_gather(local_window, 'out', axis=0, tiled=True)  74.3 us
    all_to_all x1, waiting for transfers between devices, sum_at_owner(): parts = lax.all_to_all(cut_along(array, dim, count), axis, 0, 0, tiled=True)  32 us
    all_gather x1, blocking collectives, on_device(): lax.all_gather(amplitudes, 'out', axis=0, tiled=True)  25.7 us
    all_to_all x1, starting transfers between devices, sum_at_owner(): parts = lax.all_to_all(cut_along(array, dim, count), axis, 0, 0, tiled=True)  12.3 us
    convert_element_type x1, local copies, waits for them, and re-layouts, on_device(): integral = jnp.einsum('sacp,sbdp->sabcd', left, right, preferred_element_...  11.5 us
    reshape x1, local copies, waits for them, and re-layouts, on_device(): flat = integral.reshape(slot_count * TS * TS, -1)  11.3 us
    dot_general x1, matrix products, on_device(): jnp.einsum('sacp,sbdp->sabcd', left, right, preferred_element_type=jnp.fl...  10.4 us
  transfers between devices with their start and end apart: 6, of which 6 were waited for; matrix products, arithmetic and copies ran while one was open for 1% of the time, Pallas kernels for 0%

commit v1 on v0

--- a/solution.py
+++ b/solution.py
@@ -11,7 +11,8 @@
 def broadcast_by_axis(array, axes, root):
     array = jnp.where(lax.axis_index(axes) == root, array, jnp.zeros_like(array))
     for axis in axes:
-        array = lax.psum(array, axis)
+        shards = lax.all_gather(array, axis, axis=0, tiled=False)
+        array = shards.sum(axis=0)
     return array
 
 

time: 419 us -> 358 us (0.85)
  waiting for transfers between devices: 309 us -> 231 us
  blocking collectives: 25.7 us -> 41 us
  other arithmetic: 2.78 us -> 7.01 us
    psum x2 -> x0, waiting for transfers between devices: 189 us -> none  [broadcast_by_axis(): array = lax.psum(array, axis)]
    all_gather x0 -> x1, waiting for transfers between devices: none -> 78.7 us  [broadcast_by_axis(): shards = lax.all_gather(array, axis, axis=0, tiled=False)]
    all_gather x1, waiting for transfers between devices: 4.89 us -> 37.2 us  [on_device(): lax.all_gather(chol, 'out', axis=0, tiled=True)]
    all_gather x1, blocking collectives: 25.7 us -> 34.4 us  [on_device(): lax.all_gather(amplitudes, 'out', axis=0, tiled=True)]
    all_gather x0 -> x1, blocking collectives: none -> 6.59 us  [broadcast_by_axis(): shards = lax.all_gather(array, axis, axis=0, tiled=False)]
    reduce_sum x0 -> x2, other arithmetic: none -> 4.2 us  [broadcast_by_axis(): array = shards.sum(axis=0)]
  transfers between devices with their start and end apart: 6 -> 5, of which waited for: 6 -> 5; matrix products, arithmetic and copies ran while one was open for 1% -> 2% of each run, Pallas kernels for 0% -> 0%
where the time goes in v1:
time: 358 us; the launch traced here: 357 us
  waiting for transfers between devices  231 us (65%)
  blocking collectives  41 us (11%)
  local copies, waits for them, and re-layouts  34.5 us (10%)
  starting transfers between devices  19.2 us (5%)
  between operations  13.2 us (4%)
  matrix products  11.2 us (3%)
  other arithmetic  7.01 us (2%)
    all_gather x1, waiting for transfers between devices, broadcast_by_axis(): shards = lax.all_gather(array, axis, axis=0, tiled=False)  78.7 us
    all_gather x1, waiting for transfers between devices, on_device(): lax.all_gather(local_window, 'out', axis=0, tiled=True)  74 us
    all_gather x1, waiting for transfers between devices, on_device(): lax.all_gather(chol, 'out', axis=0, tiled=True)  37.2 us
    all_gather x1, blocking collectives, on_device(): lax.all_gather(amplitudes, 'out', axis=0, tiled=True)  34.4 us
    all_to_all x1, waiting for transfers between devices, sum_at_owner(): parts = lax.all_to_all(cut_along(array, dim, count), axis, 0, 0, tiled=True)  32 us
    all_to_all x1, starting transfers between devices, sum_at_owner(): parts = lax.all_to_all(cut_along(array, dim, count), axis, 0, 0, tiled=True)  12.3 us
    convert_element_type x1, local copies, waits for them, and re-layouts, on_device(): integral = jnp.einsum('sacp,sbdp->sabcd', left, right, preferred_element_...  11.4 us
    reshape x1, local copies, waits for them, and re-layouts, on_device(): flat = integral.reshape(slot_count * TS * TS, -1)  11.3 us
  transfers between devices with their start and end apart: 5, of which 5 were waited for; matrix products, arithmetic and copies ran while one was open for 2% of the time, Pallas kernels for 0%

profile of v1, /device:TPU:1, one launch (start us, length us, event | category | flops | bytes accessed | tf_op | source)
XLA Modules:
  0.0 357.3 jit_solution(112418371662182392)
XLA Ops:
  6.5 0.0 copy-start
  6.5 0.0 all-gather.10.cloned.1.call-start
  6.5 1.8 broadcast_select_fusion
  8.3 0.0 all-gather.10.cloned.1.call-update
  8.3 0.0 all-gather.8.cloned.1.call-start
  8.4 0.7 all-gather.8.cloned.1.call-update
  9.1 0.0 all-gather.6.cloned.1.call-start
  9.1 78.7 %all-gather.10.cloned.1.call-done = bf16[128,32,640]{2,1,0:T(8,128)(2,1)} async-done(((bf16[8,32,640]{2,1,0:T(8,128)(2,1)}), bf16[128,32,640]{2,1,0:T(8,128)(2,1)}) %all-gather.10.cloned.1.call-update) | async-done | bytes 5242896 | tf_op jit(solution)/shard_map/all_gather | solution.py:14
  87.8 0.0 copy-start.1
  87.8 3.3 reduce_sum.33
  91.1 6.6 %all-gather.1 = bf16[16,32,640]{2,1,0:T(8,128)(2,1)S(1)} all-gather(bf16[8,32,640]{2,1,0:T(8,128)(2,1)S(1)} %reduce_sum.33), channel_id=3, replica_groups=mesh['contract_0'=16,'contract_1'=2,'out'=16] {'contract_1'}, dimensions={0}, use_global_device_ids=true | all-gather | bytes 983040 | tf_op jit(solution)/shard_map/all_gather | solution.py:14
  97.7 0.9 reduce_sum.34
  98.6 0.0 all-gather.6.cloned.1.call-update
  98.6 0.0 copy-done
  98.6 0.1 constant_dynamic-slice_fusion
  98.7 0.0 copy-done.1
  98.7 34.4 %all_gather.27 = bf16[128,1024]{1,0:T(8,128)(2,1)S(1)} all-gather(bf16[8,1024]{1,0:T(8,128)(2,1)S(1)} %copy-done.1), channel_id=1, replica_groups=mesh['contract_0'=16,'contract_1'=2,'out'=16] {'out'}, dimensions={0}, use_global_device_ids=true | all-gather | bytes 278528 | tf_op jit(solution)/shard_map/all_gather | solution.py:60
  133.2 37.2 %all-gather.8.cloned.1.call-done = bf16[128,32,640]{2,1,0:T(8,128)(2,1)} async-done(((bf16[8,32,640]{2,1,0:T(8,128)(2,1)}), bf16[128,32,640]{2,1,0:T(8,128)(2,1)}) %all-gather.8.cloned.1.call-update) | async-done | bytes 5242896 | tf_op jit(solution)/shard_map/all_gather | solution.py:58
  170.3 3.5 gather_fusion.1
  173.8 74.0 %all-gather.6.cloned.1.call-done = bf16[128,32,640]{2,1,0:T(8,128)(2,1)} async-done(((bf16[8,32,640]{2,1,0:T(8,128)(2,1)}), bf16[128,32,640]{2,1,0:T(8,128)(2,1)}) %all-gather.6.cloned.1.call-update) | async-done | bytes 5242896 | tf_op jit(solution)/shard_map/all_gather | solution.py:59
  247.8 4.9 %gather_fusion = bf16[4,16,32,640]{3,2,1,0:T(8,128)(2,1)} fusion(bf16[128,32,640]{2,1,0:T(8,128)(2,1)} %all-gather.6.cloned.1.call-done, s32[4]{0:T(128)S(1)} %get-tuple-element.9), kind=kCustom, calls=%fused_computation | custom fusion | bytes 5242928 | tf_op jit(solution)/shard_map/vmap()/gather | solution.py:48
  252.7 10.3 %convert_bitcast_fusion = bf16[4,16,16,32,32]{3,4,1,2,0:T(8,128)(2,1)} fusion(bf16[4,16,32,640]{3,2,1,0:T(8,128)(2,1)S(1)} %gather_fusion.1, bf16[4,16,32,640]{3,2,1,0:T(8,128)(2,1)} %gather_fusion), kind=kOutput, calls=%fused_computation.4 | convolution fusion | flops 1343225856 | bytes 7340032 | tf_op jit(solution)/shard_map/sacp,sbdp->sabcd/dot_general | solution.py:67
  263.0 11.4 %copy.9 = bf16[4,16,16,32,32]{4,3,2,1,0:T(8,128)(2,1)} copy(bf16[4,16,16,32,32]{3,4,1,2,0:T(8,128)(2,1)} %convert_bitcast_fusion) | data formatting | bytes 4194304 | tf_op jit(solution)/shard_map/convert_element_type | solution.py:69
  274.5 11.3 %reshape.26 = bf16[1024,1024]{1,0:T(8,128)(2,1)S(1)} reshape(bf16[4,16,16,32,32]{4,3,2,1,0:T(8,128)(2,1)} %copy.9) | data formatting | bytes 4194304 | tf_op jit(solution)/shard_map/reshape | solution.py:70
  285.8 0.0 copy-start.2
  285.8 0.8 convolution_bitcast_fusion
  286.7 0.0 copy-start.3
  286.7 0.9 reshape.27
  287.6 12.3 %all-to-all-start = ((f32[32,4,1024]{2,1,0:T(4,128)}), f32[32,4,1024]{2,1,0:T(4,128)S(1)}, u32[]{:S(2)}, u32[]{:S(2)}) async-start(f32[32,4,1024]{2,1,0:T(4,128)} %reshape.27), calls=%async_computation | async-start | bytes 1048576 | tf_op jit(solution)/shard_map/all_to_all | solution.py:26
  299.9 0.0 copy-done.2
  300.0 0.1 compare_and_fusion
  300.0 32.0 %all-to-all-done = f32[32,4,1024]{2,1,0:T(4,128)S(1)} async-done(((f32[32,4,1024]{2,1,0:T(4,128)}), f32[32,4,1024]{2,1,0:T(4,128)S(1)}, u32[]{:S(2)}, u32[]{:S(2)}) %all-to-all-start) | async-done | bytes 524320 | tf_op jit(solution)/shard_map/all_to_all | solution.py:26
  332.1 0.1 reduce_sum.35
  332.2 0.1 reshape.28
  332.3 0.6 gather_fusion.2
  332.9 0.1 select_bitcast_fusion
  332.9 0.1 copy.11
  333.1 0.1 broadcast_in_dim.41
  333.2 0.8 broadcast_in_dim.42
  333.9 6.8 %all-to-all-start.1 = ((f32[16,4,4,256]{3,2,1,0:T(4,128)}), f32[16,4,4,256]{3,2,1,0:T(4,128)S(1)}, u32[]{:S(2)}, u32[]{:S(2)}) async-start(f32[16,4,4,256]{3,2,1,0:T(4,128)} %broadcast_in_dim.42), calls=%async_computation.1 | async-start | bytes 524288 | tf_op jit(solution)/shard_map/all_to_all | solution.py:38
  340.8 0.0 copy-done.3
  340.8 0.1 compare_and_fusion.1
  340.9 0.1 reshape.65
  341.0 8.5 %all-to-all-done.1 = f32[16,4,4,256]{3,2,1,0:T(4,128)S(1)} async-done(((f32[16,4,4,256]{3,2,1,0:T(4,128)}), f32[16,4,4,256]{3,2,1,0:T(4,128)S(1)}, u32[]{:S(2)}, u32[]{:S(2)}) %all-to-all-start.1) | async-done | bytes 262176 | tf_op jit(solution)/shard_map/all_to_all | solution.py:38
  349.5 0.6 gather_fusion.3
  350.0 0.7 copy_add_fusion
  (3 shorter events, 0.0 us)
Async XLA Ops:
  6.5 92.1 %copy-start = (s32[64,2]{0,1:T(2,128)S(1)}, s32[64,2]{0,1:T(2,128)}, u32[]{:S(2)}) copy-start(s32[64,2]{0,1:T(2,128)} %param.7) | copy-start | bytes 1540
  6.5 81.3 %all-gather.10.cloned.1.call-start = ((), (), s32[]{:S(2)}) async-start(), calls=%async_computation.4 | async-start | bytes 5570560 | tf_op jit(solution)/shard_map/all_gather | solution.py:14
  8.3 162.0 %all-gather.8.cloned.1.call-start = ((), (), s32[]{:S(2)}) async-start(), calls=%async_computation.3 | async-start | bytes 5570560 | tf_op jit(solution)/shard_map/all_gather | solution.py:58
  9.1 238.7 %all-gather.6.cloned.1.call-start = ((), (), s32[]{:S(2)}) async-start(), calls=%async_computation.2 | async-start | bytes 5570560 | tf_op jit(solution)/shard_map/all_gather | solution.py:59
  87.8 10.9 %copy-start.1 = (bf16[8,1024]{1,0:T(8,128)(2,1)S(1)}, bf16[8,1024]{1,0:T(8,128)(2,1)}, u32[]{:S(2)}) copy-start(bf16[8,1024]{1,0:T(8,128)(2,1)} %param.6) | copy-start | bytes 49156
  285.8 14.1 %copy-start.2 = (s32[128]{0:T(128)S(1)}, s32[128]{0:T(128)}, u32[]{:S(2)}) copy-start(s32[128]{0:T(128)} %param.9) | copy-start | bytes 1540
  286.7 54.1 %copy-start.3 = (s32[64]{0:T(128)S(1)}, s32[64]{0:T(128)}, u32[]{:S(2)}) copy-start(s32[64]{0:T(128)} %param.8) | copy-start | bytes 772
  287.6 44.5 %all-to-all-start = ((f32[32,4,1024]{2,1,0:T(4,128)}), f32[32,4,1024]{2,1,0:T(4,128)S(1)}, u32[]{:S(2)}, u32[]{:S(2)}) async-start(f32[32,4,1024]{2,1,0:T(4,128)} %reshape.27), calls=%async_computation | async-start | bytes 1048576 | tf_op jit(solution)/shard_map/all_to_all | solution.py:26
  333.9 15.5 %all-to-all-start.1 = ((f32[16,4,4,256]{3,2,1,0:T(4,128)}), f32[16,4,4,256]{3,2,1,0:T(4,128)S(1)}, u32[]{:S(2)}, u32[]{:S(2)}) async-start(f32[16,4,4,256]{3,2,1,0:T(4,128)} %broadcast_in_dim.42), calls=%async_computation.1 | async-start | bytes 524288 | tf_op jit(solution)/shard_map/all_to_all | solution.py:38
Sparse Core Ops, SparseCore 0:
  9.4 78.3 all-gather.9
  91.1 79.1 all-gather.7
  173.6 74.1 all-gather.5
